TPU v7x, 256 devices: a 4x2x16 block of a 4x16x16 slice. The times are simulated.
256 devices in a mesh: grp: 2 (over y), slab: 16 (over z), blk: 4 (over x), sub: 2 (over core).
Axes of the slice: x: 4, y: 2, z: 16, core: 2. Of those that a mesh axis runs over, the one named last changes fastest.
The devices are a block of a 4x16x16 slice.
Arguments:
- cell_x: int32 [65536], P(('grp', 'slab', 'blk', 'sub')), parts along dimension 0, may hold values from 0 to 63
- cell_y: int32 [65536], P(('grp', 'slab', 'blk', 'sub')), parts along dimension 0, may hold values from 0 to 127
- cell_z: int32 [65536], P(('grp', 'slab', 'blk', 'sub')), parts along dimension 0, may hold values from 0 to 127
- offsets: float32 [3, 65536], P(None, ('grp', 'slab', 'blk', 'sub')), parts along dimension 1, may hold values from 0 to 1
- charge: float32 [65536], P(('grp', 'slab', 'blk', 'sub')), parts along dimension 0, may hold values from -4 to 4
- block_count: int32 [256], P(('grp', 'slab', 'blk', 'sub')), parts along dimension 0, may hold values from 0 to 256, as said below
- level_amplitude: float32 [4], replicated, may hold values from 0.5 to 2
- density: float32 [512, 256, 256], P(('grp', 'slab'), 'blk', 'sub'), parts along dimension 0, may hold values from 0.3 to 8.2
Outputs:
- field: float32 [512, 256, 256], P(('grp', 'slab'), 'blk', 'sub'), parts along dimension 0
- energy: float32 [2], P('grp'), parts along dimension 0
There are 2 independent parts, one for each index of `grp`. A program takes and returns all parts, laid end to end along the dimension named above; an argument that names none is the same for every part. Nothing has to cross between parts.
Inputs may be any that keep to these rules, and one draw needn't show every extreme that they name: `block_count`: within the 1 block of each device, blocks with a nonzero count come before blocks with count 0; some device has every block full.
All inputs are finite; a program needn't handle non-finite values.
Results may differ from a plain program's by a relative error of at most 0.0021.
Values sent between devices are 32-bit elements; how exact they have to be, the bound alone decides.
A program may use at most 64 MiB of HBM per device.

v0:
```python
import functools
import jax
import jax.numpy as jnp
from jax import lax
from jax.sharding import PartitionSpec as P

G0X = 64
G0Y = 128
G0Z = 128
FINE_X = 256
FINE_Y = 256
FINE_Z = 256
BQ = 256
spread_width = 1.25


def rows_first(arrays, axis, dims):
    turned = [jnp.moveaxis(a, dim, 0) for a, dim in zip(arrays, dims)]
    both = jnp.concatenate([t.reshape(len(t), -1) for t in turned], axis=1)
    out, at, gathered = (lax.all_gather(both, axis, axis=0, tiled=True), 0, [])
    for t, dim in zip(turned, dims):
        share = out[:, at : at + t[0].size].reshape(-1, *t.shape[1:])
        gathered.append(jnp.moveaxis(share, 0, dim))
        at += t[0].size
    return tuple(gathered)


def over_pieces(value, axis):
    return lax.all_gather(value, axis).sum(0)


def passed_along(value, axis, by):
    peers = lax.axis_size(axis)
    return lax.ppermute(value, axis, [(i, (i + by) % peers) for i in range(peers)])


def by_axis(value, axes):
    return functools.reduce(lax.psum, axes, value)


def axis_weights(shifts, base, coarse):
    position = shifts * (coarse / base)
    nodes = jnp.arange(coarse, dtype=jnp.float32)
    distance = nodes[None, :] - position[:, None]
    distance = distance - coarse * jnp.floor(distance / coarse + 0.5)
    return jnp.exp(-0.5 * (distance / spread_width) ** 2)


def placed_weights(placed, base, coarse, first, count):
    position = placed * (coarse / base)
    nodes = first.astype(jnp.float32) + jnp.arange(count, dtype=jnp.float32)
    distance = nodes[None, :] - position[:, None]
    distance = distance - coarse * jnp.floor(distance / coarse + 0.5)
    return jnp.exp(-0.5 * (distance / spread_width) ** 2)


def level_dims():
    return [
        (G0X * (4 - factor) // 4, G0Y * (4 - factor) // 4, G0Z * (4 - factor) // 4)
        for factor in range(4)
    ]


def spread_slab(totals, pieces, slab_index, slab_count):
    weighted, placed_x, placed_y, placed_z = pieces
    result = []
    for total, (dim_x, dim_y, dim_z) in zip(totals, level_dims()):
        slab_rows = dim_x // slab_count
        along_x = placed_weights(placed_x, G0X, dim_x, slab_index * slab_rows, slab_rows)
        along_y = axis_weights(placed_y, G0Y, dim_y)
        along_z = axis_weights(placed_z, G0Z, dim_z)
        planes = (
            ((weighted[:, None] * along_x)[:, :, None] * along_y[:, None, :])
            .reshape(weighted.shape[0], slab_rows * dim_y)
            .astype(jnp.bfloat16)
        )
        result.append(
            total
            + lax.dot_general(
                planes,
                along_z.astype(jnp.bfloat16),
                (((0,), (0,)), ((), ())),
                preferred_element_type=jnp.float32,
            )
        )
    return tuple(result)


def hat_matrix(fine, coarse, first_row, rows):
    fine_rows = first_row + jnp.arange(rows, dtype=jnp.int32)
    nodes = jnp.arange(coarse, dtype=jnp.int32)
    period = coarse * fine
    moved = (nodes[None, :] * fine - fine_rows[:, None] * coarse) % period
    moved = jnp.where(moved * 2 >= period, moved - period, moved)
    distance = moved.astype(jnp.float32) / fine
    return jnp.maximum(0.0, 1.0 - jnp.abs(distance))


def local_hat(fine_rows, coarse_cols, coarse):
    row_ids = jnp.arange(fine_rows, dtype=jnp.int32)
    col_ids = jnp.arange(coarse_cols, dtype=jnp.int32)
    moved = col_ids[None, :] * FINE_X - row_ids[:, None] * coarse
    distance = moved.astype(jnp.float32) / FINE_X
    return jnp.maximum(0.0, 1.0 - jnp.abs(distance))


def interpolate(mat_x, mat_y, mat_z, cube):
    highest = lax.Precision.HIGHEST
    first = jnp.einsum("ax,xyz->ayz", mat_x, cube, precision=highest)
    second = jnp.einsum("by,ayz->abz", mat_y, first, precision=highest)
    return jnp.einsum("cz,abz->abc", mat_z, second, precision=highest)


def on_device(cell_x, cell_y, cell_z, offsets, charge, block_count, level_amplitude, density):
    blocks = block_count.shape[0]
    live = (jnp.arange(BQ, dtype=jnp.int32)[None, :] < block_count[:, None]).astype(jnp.float32)
    weighted = charge.reshape(blocks, BQ) * live
    slab_count = lax.axis_size("slab")
    slab_index = lax.axis_index("slab")
    placed_x = cell_x.astype(jnp.float32) + offsets[0]
    placed_y = cell_y.astype(jnp.float32) + offsets[1]
    placed_z = cell_z.astype(jnp.float32) + offsets[2]
    flat_weighted = weighted.reshape(-1)
    begin = tuple(
        (
            jnp.zeros((dim_x // slab_count * dim_y, dim_z), jnp.float32)
            for dim_x, dim_y, dim_z in level_dims()
        )
    )
    totals = begin
    pieces = rows_first((flat_weighted, placed_x, placed_y, placed_z), "slab", (0, 0, 0, 0))
    spread_rows = pieces[0].shape[0]
    full = spread_rows // BQ

    def one_block(number, carried):
        block = tuple((lax.dynamic_slice_in_dim(array, number * BQ, BQ) for array in pieces))
        return spread_slab(carried, block, slab_index, slab_count)

    totals = lax.fori_loop(0, full, one_block, totals)
    summed = jax.tree.map(lambda part: over_pieces(part, ("blk", "sub")), totals)
    slabs = tuple(
        (
            rows.reshape(dim_x // slab_count, dim_y, dim_z)
            for rows, (dim_x, dim_y, dim_z) in zip(summed, level_dims())
        )
    )
    firsts = tuple((piece[0:1] for piece in slabs))
    after = passed_along(firsts, "slab", -1)
    rows_x, rows_y, rows_z = density.shape
    blk_start = lax.axis_index("blk") * rows_y
    sub_start = lax.axis_index("sub") * rows_z
    field = jnp.zeros((rows_x, rows_y, rows_z), jnp.float32)
    for factor, (dim_x, dim_y, dim_z) in enumerate(level_dims()):
        extended = jnp.concatenate([slabs[factor], after[factor]], axis=0)
        mat_x = local_hat(rows_x, dim_x // slab_count + 1, dim_x)
        mat_y = hat_matrix(FINE_Y, dim_y, blk_start, rows_y)
        mat_z = hat_matrix(FINE_Z, dim_z, sub_start, rows_z)
        field = field + level_amplitude[factor] * interpolate(mat_x, mat_y, mat_z, extended)
    total = by_axis(jnp.sum(density * field), ("slab", "blk", "sub"))
    energy = (total / (FINE_X * FINE_Y * FINE_Z)).reshape(1)
    return (field, energy)


def solution(mesh):
    in_specs = (
        P(("grp", "slab", "blk", "sub")),
        P(("grp", "slab", "blk", "sub")),
        P(("grp", "slab", "blk", "sub")),
        P(None, ("grp", "slab", "blk", "sub")),
        P(("grp", "slab", "blk", "sub")),
        P(("grp", "slab", "blk", "sub")),
        P(),
        P(("grp", "slab"), "blk", "sub"),
    )
    out_specs = (P(("grp", "slab"), "blk", "sub"), P("grp"))
    return jax.shard_map(
        on_device, mesh=mesh, in_specs=in_specs, out_specs=out_specs, check_vma=False
    )
```

profile of v0, /device:TPU:33, one launch (start us, length us, event | category | flops | bytes accessed | tf_op | source)
XLA Modules:
  0.0 214.6 jit_solution(13088567531267280203)
XLA Ops:
  7.3 0.8 fusion.396
  8.7 0.7 convert_add_fusion.2
  9.4 0.7 convert_add_fusion.1
  10.1 0.7 convert_add_fusion
  10.8 0.7 compare_select_fusion
  11.5 42.4 %all_gather.27 = f32[4096,4]{0,1:T(4,128)S(1)} all-gather(f32[256,4]{0,1:T(4,128)S(1)} %pad_maximum_fusion), channel_id=1, replica_groups=mesh['grp'=2,'slab'=16,'blk'=4,'sub'=2] {'slab'}, dimensions={0}, use_global_device_ids=true | all-gather | bytes 69632 | tf_op jit(solution)/shard_map/all_gather | solution.py:20
  54.0 35.3 %while.22 = (s32[]{:T(128)}, f32[512,128]{1,0:T(8,128)S(1)}, f32[288,96]{1,0:T(8,128)S(1)}, f32[128,64]{0,1:T(8,128)S(1)}, f32[32,32]{1,0:T(8,128)S(1)}, /*index...) while((s32[]{:T(128)}, f32[512,128]{1,0:T(8,128)S(1)}, ...), condition=%wide.region_1.0_spmd.clone, body=%wide.region_0.0_spmd.clone.sunk | while | flops 54709520 | bytes 2422072 | solution.py:139
  54.9 0.4 convolution_add_fusion.8
  57.1 0.4 convolution_add_fusion.8
  59.0 0.3 multiply_convert_fusion.10
  59.3 0.4 convolution_add_fusion.8
  61.2 0.3 multiply_convert_fusion.10
  61.5 0.4 convolution_add_fusion.8
  63.8 0.4 convolution_add_fusion.8
  66.0 0.4 convolution_add_fusion.8
  68.2 0.4 convolution_add_fusion.8
  70.4 0.4 convolution_add_fusion.8
  72.6 0.4 convolution_add_fusion.8
  74.8 0.4 convolution_add_fusion.8
  77.0 0.4 convolution_add_fusion.8
  79.2 0.4 convolution_add_fusion.8
  81.4 0.4 convolution_add_fusion.8
  83.6 0.4 convolution_add_fusion.8
  85.8 0.4 convolution_add_fusion.8
  88.0 0.4 convolution_add_fusion.8
  89.3 0.7 copy-done.1
  90.1 23.4 %all-gather.1 = f32[2304,96]{1,0:T(8,128)S(1)} all-gather(f32[288,96]{1,0:T(8,128)S(1)} %get-tuple-element.257), channel_id=3, replica_groups=mesh['grp'=2,'slab'=16,'blk'=4,'sub'=2] {'blk','sub'}, dimensions={0}, use_global_device_ids=true | all-gather | bytes 995328 | tf_op jit(solution)/shard_map/all_gather | solution.py:29
  113.8 13.0 %all-gather.3 = f32[256,32]{1,0:T(8,128)S(1)} all-gather(f32[32,32]{1,0:T(8,128)S(1)} %get-tuple-element.259), channel_id=5, replica_groups=mesh['grp'=2,'slab'=16,'blk'=4,'sub'=2] {'blk','sub'}, dimensions={0}, use_global_device_ids=true | all-gather | bytes 36864 | tf_op jit(solution)/shard_map/all_gather | solution.py:29
  126.9 13.1 %all-gather.2 = f32[1024,64]{0,1:T(8,128)S(1)} all-gather(f32[128,64]{0,1:T(8,128)S(1)} %get-tuple-element.258), channel_id=4, replica_groups=mesh['grp'=2,'slab'=16,'blk'=4,'sub'=2] {'blk','sub'}, dimensions={0}, use_global_device_ids=true | all-gather | bytes 294912 | tf_op jit(solution)/shard_map/all_gather | solution.py:29
  140.6 0.6 fusion.397
  141.6 0.5 fusion.144
  142.1 0.6 convolution_bitcast_fusion.3
  142.8 1.7 convolution_multiply_fusion
  144.4 0.7 fusion.87
  145.2 1.1 convolution_bitcast_fusion
  146.2 1.0 fusion.83
  147.2 1.7 reduce_sum.45
  149.0 1.2 collective-permute-start
  150.1 0.9 convolution_bitcast_fusion.1
  151.2 1.8 collective-permute-done
  153.1 1.2 fusion.77
  154.2 1.0 convolution_bitcast_fusion.2
  155.3 1.3 convolution_multiply_fusion.3
  156.6 1.3 fusion.74
  157.9 3.1 %multiply_reduce_fusion = (f32[]{:T(128)}, f32[16,64,128]{2,1,0:T(8,128)}) fusion(f32[16,64,128]{2,1,0:T(8,128)S(1)} %copy-done, f32[16,64,128]{2,1,0:T(8,128)S(1)} %convolution_multiply_fusion, f32[16,64,128]{2,1,0:T(8,128)S(1)} %fusion.74, f32[16,64,64]{1,2,0:T(8,128)S(1)} %convolution_bitcast_fusion, s32[128]{0:T(128)S(1)} %fusion.309, ...), kind=kOutput, calls=%fused_computation.123 | convolution fusion | flops 101490688 | bytes 2360072 | tf_op jit(solution)/shard_map/cz,abz->abc/dot_general | solution.py:111
  161.0 23.5 %psum.21 = f32[]{:T(128)} all-reduce(f32[]{:T(128)} %get-tuple-element.354), channel_id=1, replica_groups=mesh['grp'=2,'slab'=16,'blk'=4,'sub'=2] {'slab'}, use_global_device_ids=true, to_apply=%region_7.8 | all-reduce | flops 1 | bytes 8 | tf_op jit(solution)/shard_map/psum | solution.py:38
  184.5 8.1 %psum.22 = f32[]{:T(128)} all-reduce(f32[]{:T(128)} %psum.21), channel_id=1, replica_groups=mesh['grp'=2,'slab'=16,'blk'=4,'sub'=2] {'blk'}, use_global_device_ids=true, to_apply=%region_8.9 | all-reduce | flops 1 | bytes 8 | tf_op jit(solution)/shard_map/psum | solution.py:38
  192.6 13.3 %psum.23 = f32[]{:T(128)} all-reduce(f32[]{:T(128)} %psum.22), channel_id=1, replica_groups=mesh['grp'=2,'slab'=16,'blk'=4,'sub'=2] {'sub'}, use_global_device_ids=true, to_apply=%region_9.10 | all-reduce | flops 1 | bytes 8 | tf_op jit(solution)/shard_map/psum | solution.py:38
  (382 shorter events, 29.0 us)
Async XLA Ops:
  7.2 140.1 %all-gather.6.cloned.1.call-start = ((), (), s32[]{:S(2)}) async-start(), calls=%async_computation | async-start | bytes 2359296 | tf_op jit(solution)/shard_map/all_gather | solution.py:29
  89.3 0.7 copy-start.1
  90.1 50.5 %copy-start.2 = (f32[4]{0:T(128)S(1)}, f32[4]{0:T(128)}, u32[]{:S(2)}) copy-start(f32[4]{0:T(128)} %param.16) | copy-start | bytes 52
  113.6 32.6 %collective-permute-start.1 = (f32[1,96,96]{2,0,1:T(1,128)S(1)}, f32[1,96,96]{2,0,1:T(1,128)S(1)}, u32[]{:S(2)}, u32[]{:S(2)}) collective-permute-start(f32[1,96,96]{2,0,1:T(1,128)S(1)} %bitcast.118), channel_id=1, source_target_pairs={{0,120},{8,0},{16,8},{24,16},{32,24},{40,32},{48,40},{56,48},{64,5... | collective-permute-start | bytes 110600 | tf_op jit(solution)/shard_map/ppermute | solution.py:34
  126.7 14.8 %collective-permute-start.3 = (f32[1,32,32]{2,0,1:T(1,128)S(1)}, f32[1,32,32]{2,0,1:T(1,128)S(1)}, u32[]{:S(2)}, u32[]{:S(2)}) collective-permute-start(f32[1,32,32]{2,0,1:T(1,128)S(1)} %bitcast.115), channel_id=1, source_target_pairs={{0,120},{8,0},{16,8},{24,16},{32,24},{40,32},{48,40},{56,48},{64,5... | collective-permute-start | bytes 12296 | tf_op jit(solution)/shard_map/ppermute | solution.py:34
  140.2 4.3 %collective-permute-start.2 = (f32[1,64,64]{2,0,1:T(1,128)S(1)}, f32[1,64,64]{2,0,1:T(1,128)S(1)}, u32[]{:S(2)}, u32[]{:S(2)}) collective-permute-start(f32[1,64,64]{2,0,1:T(1,128)S(1)} %bitcast.119), channel_id=1, source_target_pairs={{0,120},{8,0},{16,8},{24,16},{32,24},{40,32},{48,40},{56,48},{64,5... | collective-permute-start | bytes 49160 | tf_op jit(solution)/shard_map/ppermute | solution.py:34
  149.0 4.1 %collective-permute-start = (f32[1,128,128]{2,0,1:T(1,128)S(1)}, f32[1,128,128]{2,0,1:T(1,128)S(1)}, u32[]{:S(2)}, u32[]{:S(2)}) collective-permute-start(f32[1,128,128]{2,0,1:T(1,128)S(1)} %bitcast.117), channel_id=1, source_target_pairs={{0,120},{8,0},{16,8},{24,16},{32,24},{40,32},{48,40},{56,48},{64,5... | collective-permute-start | bytes 196616 | tf_op jit(solution)/shard_map/ppermute | solution.py:34
  154.2 3.6 %copy-start = (f32[16,64,128]{2,1,0:T(8,128)S(1)}, f32[16,64,128]{2,1,0:T(8,128)}, u32[]{:S(2)}) copy-start(f32[16,64,128]{2,1,0:T(8,128)} %param.17) | copy-start | bytes 1572868
Sparse Core Ops, SparseCore 0:
  90.2 32.4 all-gather.5
where the time goes:
time: 215 us
  blocking collectives  137 us (64%)
  matrix products  28.8 us (13%)
  other arithmetic  21.5 us (10%)
  between operations  16.9 us (8%)
  local copies, waits for them, and re-layouts  5.18 us (2%)
    all_gather x3, blocking collectives, over_pieces(): return lax.all_gather(value, axis).sum(0)  49.4 us
    psum x3, blocking collectives, by_axis(): return functools.reduce(lax.psum, axes, value)  44.9 us
    all_gather x1, blocking collectives, rows_first(): out, at, gathered = (lax.all_gather(both, axis, axis=0, tiled=True), 0, [])  42.4 us
    dot_general x64, matrix products, spread_slab(): lax.dot_general(planes, along_z.astype(jnp.bfloat16), (((0,), (0,)), ((),...  14.4 us
    dot_general x4, matrix products, interpolate(): return jnp.einsum('cz,abz->abc', mat_z, second, precision=highest)  7.4 us
    convert_element_type x48, other arithmetic, spread_slab(): planes = ((weighted[:, None] * along_x)[:, :, None] * along_y[:, None, :]...  5.89 us
    mul x64, other arithmetic, spread_slab(): weighted[:, None] * along_x  5.47 us
  transfers between devices with their start and end apart: 5, of which 1 were waited for; matrix products, arithmetic and copies ran while one was open for 4% of the time, Pallas kernels for 0%

commit v1 on v0

--- a/solution.py
+++ b/solution.py
@@ -14,10 +14,15 @@
 spread_width = 1.25
 
 
+def all_by_exchange(array, axis, dim):
+    repeated = jnp.stack([array] * lax.axis_size(axis))
+    return jnp.concatenate(lax.all_to_all(repeated, axis, 0, 0), axis=dim)
+
+
 def rows_first(arrays, axis, dims):
     turned = [jnp.moveaxis(a, dim, 0) for a, dim in zip(arrays, dims)]
     both = jnp.concatenate([t.reshape(len(t), -1) for t in turned], axis=1)
-    out, at, gathered = (lax.all_gather(both, axis, axis=0, tiled=True), 0, [])
+    out, at, gathered = (all_by_exchange(both, axis, 0), 0, [])
     for t, dim in zip(turned, dims):
         share = out[:, at : at + t[0].size].reshape(-1, *t.shape[1:])
         gathered.append(jnp.moveaxis(share, 0, dim))

time: 215 us -> 205 us (0.953)
  blocking collectives: 137 us -> 91.3 us
  starting transfers between devices: 1.76 us -> 26.4 us
  waiting for transfers between devices: 1.9 us -> 12.2 us
    all_gather x1 -> x0, blocking collectives: 42.4 us -> none  [rows_first(): out, at, gathered = (lax.all_gather(both, axis, axis=0, tiled=True), 0, [])]
    all_to_all x0 -> x1, starting transfers between devices: none -> 24.5 us  [all_by_exchange(): return jnp.concatenate(lax.all_to_all(repeated, axis, 0, 0), axis=dim)]
    all_to_all x0 -> x1, waiting for transfers between devices: none -> 11.2 us  [all_by_exchange(): return jnp.concatenate(lax.all_to_all(repeated, axis, 0, 0), axis=dim)]
    all_gather x3, blocking collectives: 49.4 us -> 44.9 us  [over_pieces(): return lax.all_gather(value, axis).sum(0)]
  transfers between devices with their start and end apart: 5 -> 6, of which waited for: 1 -> 2; matrix products, arithmetic and copies ran while one was open for 4% -> 4% of each run, Pallas kernels for 0% -> 0%
where the time goes in v1:
time: 205 us
  blocking collectives  91.3 us (45%)
  matrix products  28.7 us (14%)
  starting transfers between devices  26.4 us (13%)
  other arithmetic  21.5 us (10%)
  between operations  16.9 us (8%)
  waiting for transfers between devices  12.2 us (6%)
  local copies, waits for them, and re-layouts  5.84 us (3%)
    psum x3, blocking collectives, by_axis(): return functools.reduce(lax.psum, axes, value)  46.4 us
    all_gather x3, blocking collectives, over_pieces(): return lax.all_gather(value, axis).sum(0)  44.9 us
    all_to_all x1, starting transfers between devices, all_by_exchange(): return jnp.concatenate(lax.all_to_all(repeated, axis, 0, 0), axis=dim)  24.5 us
    dot_general x64, matrix products, spread_slab(): lax.dot_general(planes, along_z.astype(jnp.bfloat16), (((0,), (0,)), ((),...  14.4 us
    all_to_all x1, waiting for transfers between devices, all_by_exchange(): return jnp.concatenate(lax.all_to_all(repeated, axis, 0, 0), axis=dim)  11.2 us
    dot_general x4, matrix products, interpolate(): return jnp.einsum('cz,abz->abc', mat_z, second, precision=highest)  7.28 us
    convert_element_type x48, other arithmetic, spread_slab(): planes = ((weighted[:, None] * along_x)[:, :, None] * along_y[:, None, :]...  5.89 us
    mul x64, other arithmetic, spread_slab(): weighted[:, None] * along_x  5.47 us
  transfers between devices with their start and end apart: 6, of which 2 were waited for; matrix products, arithmetic and copies ran while one was open for 4% of the time, Pallas kernels for 0%

profile of v1, /device:TPU:33, one launch (start us, length us, event | category | flops | bytes accessed | tf_op | source)
XLA Modules:
  0.0 204.6 jit_solution(16818861436442328595)
XLA Ops:
  7.2 0.8 fusion.396
  8.6 0.7 convert_add_fusion.2
  9.3 0.7 convert_add_fusion.1
  10.0 0.7 convert_add_fusion
  10.7 0.7 compare_select_fusion
  11.4 0.6 stack.2
  12.0 24.5 %all-to-all-start = ((f32[16,256,4]{1,2,0:T(4,128)}), f32[16,256,4]{1,2,0:T(4,128)S(1)}, u32[]{:S(2)}, u32[]{:S(2)}) async-start(f32[16,256,4]{1,2,0:T(4,128)} %stack.2), calls=%async_computation | async-start | bytes 131072 | tf_op jit(solution)/shard_map/all_to_all | solution.py:19
  36.7 11.2 %all-to-all-done = f32[16,256,4]{1,2,0:T(4,128)S(1)} async-done(((f32[16,256,4]{1,2,0:T(4,128)}), f32[16,256,4]{1,2,0:T(4,128)S(1)}, u32[]{:S(2)}, u32[]{:S(2)}) %all-to-all-start) | async-done | bytes 65568 | tf_op jit(solution)/shard_map/all_to_all | solution.py:19
  48.0 35.3 %while.22 = (s32[]{:T(128)}, f32[512,128]{1,0:T(8,128)S(1)}, f32[288,96]{1,0:T(8,128)S(1)}, f32[128,64]{0,1:T(8,128)S(1)}, f32[32,32]{1,0:T(8,128)S(1)}, /*index...) while((s32[]{:T(128)}, f32[512,128]{1,0:T(8,128)S(1)}, ...), condition=%wide.region_1.0_spmd.clone, body=%wide.region_0.0_spmd.clone.sunk | while | flops 54709520 | bytes 2422072 | solution.py:144
  48.9 0.4 convolution_add_fusion.8
  51.1 0.4 convolution_add_fusion.8
  53.3 0.4 convolution_add_fusion.8
  55.5 0.4 convolution_add_fusion.8
  57.7 0.4 convolution_add_fusion.8
  59.9 0.4 convolution_add_fusion.8
  62.1 0.4 convolution_add_fusion.8
  64.3 0.4 convolution_add_fusion.8
  66.5 0.4 convolution_add_fusion.8
  68.7 0.4 convolution_add_fusion.8
  71.0 0.4 convolution_add_fusion.8
  73.2 0.4 convolution_add_fusion.8
  75.4 0.4 convolution_add_fusion.8
  77.6 0.4 convolution_add_fusion.8
  79.8 0.4 convolution_add_fusion.8
  82.0 0.4 convolution_add_fusion.8
  83.3 0.7 copy-done.1
  84.2 0.6 fusion.397
  84.9 17.9 %all-gather.1 = f32[2304,96]{1,0:T(8,128)S(1)} all-gather(f32[288,96]{1,0:T(8,128)S(1)} %get-tuple-element.257), channel_id=3, replica_groups=mesh['grp'=2,'slab'=16,'blk'=4,'sub'=2] {'blk','sub'}, dimensions={0}, use_global_device_ids=true | all-gather | bytes 995328 | tf_op jit(solution)/shard_map/all_gather | solution.py:34
  103.2 13.7 %all-gather.3 = f32[256,32]{1,0:T(8,128)S(1)} all-gather(f32[32,32]{1,0:T(8,128)S(1)} %get-tuple-element.259), channel_id=5, replica_groups=mesh['grp'=2,'slab'=16,'blk'=4,'sub'=2] {'blk','sub'}, dimensions={0}, use_global_device_ids=true | all-gather | bytes 36864 | tf_op jit(solution)/shard_map/all_gather | solution.py:34
  117.0 13.3 %all-gather.2 = f32[1024,64]{0,1:T(8,128)S(1)} all-gather(f32[128,64]{0,1:T(8,128)S(1)} %get-tuple-element.258), channel_id=4, replica_groups=mesh['grp'=2,'slab'=16,'blk'=4,'sub'=2] {'blk','sub'}, dimensions={0}, use_global_device_ids=true | all-gather | bytes 294912 | tf_op jit(solution)/shard_map/all_gather | solution.py:34
  131.0 0.5 fusion.144
  131.6 0.6 convolution_bitcast_fusion.3
  132.2 1.7 convolution_multiply_fusion
  133.9 0.7 fusion.87
  134.6 1.1 convolution_bitcast_fusion
  135.7 1.0 fusion.83
  136.7 1.7 reduce_sum.45
  138.4 1.2 collective-permute-start
  139.7 0.9 convolution_bitcast_fusion.1
  140.7 0.9 collective-permute-done
  141.7 1.2 fusion.77
  142.8 1.0 convolution_bitcast_fusion.2
  143.9 1.2 convolution_multiply_fusion.3
  145.1 1.3 fusion.74
  146.4 3.1 %multiply_reduce_fusion = (f32[]{:T(128)}, f32[16,64,128]{2,1,0:T(8,128)}) fusion(f32[16,64,128]{2,1,0:T(8,128)S(1)} %copy-done, f32[16,64,128]{2,1,0:T(8,128)S(1)} %convolution_multiply_fusion, f32[16,64,128]{2,1,0:T(8,128)S(1)} %fusion.74, f32[16,64,64]{1,2,0:T(8,128)S(1)} %convolution_bitcast_fusion, s32[128]{0:T(128)S(1)} %fusion.309, ...), kind=kOutput, calls=%fused_computation.123 | convolution fusion | flops 101490688 | bytes 2360072 | tf_op jit(solution)/shard_map/cz,abz->abc/dot_general | solution.py:116
  149.5 23.8 %psum.21 = f32[]{:T(128)} all-reduce(f32[]{:T(128)} %get-tuple-element.354), channel_id=1, replica_groups=mesh['grp'=2,'slab'=16,'blk'=4,'sub'=2] {'slab'}, use_global_device_ids=true, to_apply=%region_7.8 | all-reduce | flops 1 | bytes 8 | tf_op jit(solution)/shard_map/psum | solution.py:43
  173.3 8.6 %psum.22 = f32[]{:T(128)} all-reduce(f32[]{:T(128)} %psum.21), channel_id=1, replica_groups=mesh['grp'=2,'slab'=16,'blk'=4,'sub'=2] {'blk'}, use_global_device_ids=true, to_apply=%region_8.9 | all-reduce | flops 1 | bytes 8 | tf_op jit(solution)/shard_map/psum | solution.py:43
  182.0 14.0 %psum.23 = f32[]{:T(128)} all-reduce(f32[]{:T(128)} %psum.22), channel_id=1, replica_groups=mesh['grp'=2,'slab'=16,'blk'=4,'sub'=2] {'sub'}, use_global_device_ids=true, to_apply=%region_9.10 | all-reduce | flops 1 | bytes 8 | tf_op jit(solution)/shard_map/psum | solution.py:43
  (384 shorter events, 29.6 us)
Async XLA Ops:
  12.0 35.9 %all-to-all-start = ((f32[16,256,4]{1,2,0:T(4,128)}), f32[16,256,4]{1,2,0:T(4,128)S(1)}, u32[]{:S(2)}, u32[]{:S(2)}) async-start(f32[16,256,4]{1,2,0:T(4,128)} %stack.2), calls=%async_computation | async-start | bytes 131072 | tf_op jit(solution)/shard_map/all_to_all | solution.py:19
  36.5 100.1 %all-gather.6.cloned.1.call-start = ((), (), s32[]{:S(2)}) async-start(), calls=%async_computation.1 | async-start | bytes 2359296 | tf_op jit(solution)/shard_map/all_gather | solution.py:34
  48.0 36.3 %copy-start.2 = (f32[4]{0:T(128)S(1)}, f32[4]{0:T(128)}, u32[]{:S(2)}) copy-start(f32[4]{0:T(128)} %param.16) | copy-start | bytes 52
  83.3 0.7 copy-start.1
  103.0 32.7 %collective-permute-start.1 = (f32[1,96,96]{2,0,1:T(1,128)S(1)}, f32[1,96,96]{2,0,1:T(1,128)S(1)}, u32[]{:S(2)}, u32[]{:S(2)}) collective-permute-start(f32[1,96,96]{2,0,1:T(1,128)S(1)} %bitcast.120), channel_id=1, source_target_pairs={{0,120},{8,0},{16,8},{24,16},{32,24},{40,32},{48,40},{56,48},{64,5... | collective-permute-start | bytes 110600 | tf_op jit(solution)/shard_map/ppermute | solution.py:39
  116.9 14.1 %collective-permute-start.3 = (f32[1,32,32]{2,0,1:T(1,128)S(1)}, f32[1,32,32]{2,0,1:T(1,128)S(1)}, u32[]{:S(2)}, u32[]{:S(2)}) collective-permute-start(f32[1,32,32]{2,0,1:T(1,128)S(1)} %bitcast.117), channel_id=1, source_target_pairs={{0,120},{8,0},{16,8},{24,16},{32,24},{40,32},{48,40},{56,48},{64,5... | collective-permute-start | bytes 12296 | tf_op jit(solution)/shard_map/ppermute | solution.py:39
  130.7 3.1 %collective-permute-start.2 = (f32[1,64,64]{2,0,1:T(1,128)S(1)}, f32[1,64,64]{2,0,1:T(1,128)S(1)}, u32[]{:S(2)}, u32[]{:S(2)}) collective-permute-start(f32[1,64,64]{2,0,1:T(1,128)S(1)} %bitcast.121), channel_id=1, source_target_pairs={{0,120},{8,0},{16,8},{24,16},{32,24},{40,32},{48,40},{56,48},{64,5... | collective-permute-start | bytes 49160 | tf_op jit(solution)/shard_map/ppermute | solution.py:39
  138.4 3.2 %collective-permute-start = (f32[1,128,128]{2,0,1:T(1,128)S(1)}, f32[1,128,128]{2,0,1:T(1,128)S(1)}, u32[]{:S(2)}, u32[]{:S(2)}) collective-permute-start(f32[1,128,128]{2,0,1:T(1,128)S(1)} %bitcast.119), channel_id=1, source_target_pairs={{0,120},{8,0},{16,8},{24,16},{32,24},{40,32},{48,40},{56,48},{64,5... | collective-permute-start | bytes 196616 | tf_op jit(solution)/shard_map/ppermute | solution.py:39
  142.8 3.6 %copy-start = (f32[16,64,128]{2,1,0:T(8,128)S(1)}, f32[16,64,128]{2,1,0:T(8,128)}, u32[]{:S(2)}) copy-start(f32[16,64,128]{2,1,0:T(8,128)} %param.17) | copy-start | bytes 1572868
Sparse Core Ops, SparseCore 0:
  84.2 26.9 all-gather.5
